TPU v7x, 32 devices: a whole 2x2x4 slice. The times are simulated.
32 devices in a mesh: dp: 8 (over z, y), tensor: 4 (over x, core).
Axes of the slice: x: 2, y: 2, z: 4, core: 2. Of those that a mesh axis runs over, the one named last changes fastest.
Arguments:
- tokens: bfloat16 [16384, 4096], P('dp', 'tensor'), may hold values from -6 to 6
- cotangent: bfloat16 [16384, 1536], P('dp', 'tensor'), may hold values from -0.059814453 to 0.059814453
- seg_start: int32 [8, 2], P('dp'), may hold values from 0 to 1024, as said below
- seg_length: int32 [8, 2], P('dp'), may hold values from 0 to 1024, as said below
Outputs:
- weight_grad: float32 [4096, 2, 1536], P('dp', None, 'tensor')
Inputs may be any that keep to these rules, and one draw needn't show every extreme that they name: Within each index of dp the 2 segments lie in expert order, packed from row 0 without gaps: seg_start is the running sum of seg_length before each expert. `seg_length`: each length is at most 1024; in every draw some expert on some index of dp has exactly 1024 rows. Rows after the last segment belong to no expert.
All inputs are finite; a program needn't handle non-finite values.
Results may differ from a plain program's by a relative error of at most 0.0003.
Values may be sent and summed in bfloat16 or wider, within the bound.
A program may use at most 128 MiB of HBM per device.

v0:
```python
import jax
import jax.numpy as jnp
from jax import lax
from jax.sharding import PartitionSpec as P

E_W = 2
CAP = 1024


def block_term(columns, grads, lower, upper, size):
    total_rows = columns.shape[0]
    first = jnp.minimum(lower, total_rows - size)
    rows = first + jnp.arange(size, dtype=jnp.int32)
    keep = (rows >= lower) & (rows < upper)
    block_x = lax.dynamic_slice_in_dim(columns, first, size, 0)
    block_g = lax.dynamic_slice_in_dim(grads, first, size, 0)
    block_g = jnp.where(keep[:, None], block_g, jnp.zeros_like(block_g))
    return lax.dot_general(
        block_x, block_g, (((0,), (0,)), ((), ())), preferred_element_type=jnp.float32
    )


def expert_term(columns, grads, start, length):
    return block_term(columns, grads, start, start + length, CAP)


def all_experts(columns, grads, seg_start, seg_length):
    terms = [
        expert_term(columns, grads, seg_start[0, expert], seg_length[0, expert])
        for expert in range(E_W)
    ]
    return jnp.stack(terms, 1)


def per_device(tokens, cotangent, seg_start, seg_length):
    whole = lax.all_gather(tokens, "tensor", axis=1, tiled=True)
    terms = all_experts(whole, cotangent, seg_start, seg_length)
    return lax.psum_scatter(terms, "dp", scatter_dimension=0, tiled=True)


def solution(mesh):
    in_specs = (P("dp", "tensor"), P("dp", "tensor"), P("dp", None), P("dp", None))
    out_specs = P("dp", None, "tensor")
    return jax.shard_map(
        per_device, mesh=mesh, in_specs=in_specs, out_specs=out_specs, check_vma=False
    )
```

profile of v0, /device:TPU:0, one launch (start us, length us, event | category | flops | bytes accessed | tf_op | source)
XLA Modules:
  0.0 359.5 jit_solution(8226653060245499362)
XLA Ops:
  6.5 0.0 all-gather.2.cloned.1.call-start
  6.5 0.7 all-gather.2.cloned.1.call-update
  7.3 0.0 reduce-scatter.2.cloned.1.call-start
  7.3 1.4 fusion.29
  10.0 1.3 fusion.28
  13.9 0.7 fusion.22
  14.5 0.7 fusion.23
  15.2 102.3 %all-gather.2.cloned.1.call-done = bf16[2048,4096]{1,0:T(8,128)(2,1)} async-done(((bf16[2048,1024]{1,0:T(8,128)(2,1)}), bf16[2048,4096]{1,0:T(8,128)(2,1)}) %all-gather.2.cloned.1.call-update) | async-done | bytes 16777232 | tf_op jit(solution)/shard_map/all_gather | solution.py:36
  117.5 0.0 copy-start
  117.5 0.0 copy-start.1
  117.5 7.5 %fusion.7 = f32[4096,1,384]{2,0,1:T(8,128)S(1)} fusion(bf16[2048,4096]{1,0:T(8,128)(2,1)} %all-gather.2.cloned.1.call-done, s32[]{:T(128)S(6)} %select_n.17, bf16[2048,384]{1,0:T(8,128)(2,1)} %param.5, pred[1024]{0:T(1024)(128)(4,1)S(1)} %fusion.23), kind=kOutput, calls=%fused_computation.6 | convolution fusion | flops 3221618688 | bytes 15468544 | tf_op jit(solution)/shard_map/dot_general | solution.py:18
  125.1 0.9 copy-done
  126.0 0.4 copy-done.1
  126.4 6.7 %fusion.4 = f32[4096,1,384]{2,0,1:T(8,128)} fusion(bf16[2048,4096]{1,0:T(8,128)(2,1)S(1)} %copy-done, s32[]{:T(128)S(6)} %select_n.15, bf16[2048,384]{1,0:T(8,128)(2,1)S(1)} %copy-done.1, pred[1024]{0:T(1024)(128)(4,1)S(1)} %fusion.22), kind=kOutput, calls=%fused_computation.5 | convolution fusion | flops 3221618688 | bytes 15468544 | tf_op jit(solution)/shard_map/dot_general | solution.py:18
  133.1 8.1 %pad_maximum_fusion = f32[4096,2,384]{2,0,1:T(8,128)} fusion(f32[4096,1,384]{2,0,1:T(8,128)S(1)} %fusion.7, f32[4096,1,384]{2,0,1:T(8,128)} %fusion.4), kind=kLoop, calls=%fused_computation | loop fusion | flops 3145728 | bytes 25165824 | tf_op jit(solution)/shard_map/stack | solution.py:32
  141.2 0.0 reduce-scatter.2.cloned.1.call-update
  141.3 207.6 %reduce-scatter.2.cloned.1.call-done = f32[512,2,384]{2,0,1:T(8,128)} async-done(((f32[4096,2,384]{2,0,1:T(8,128)}), f32[512,2,384]{2,0,1:T(8,128)}) %reduce-scatter.2.cloned.1.call-update) | async-done | bytes 1572880 | tf_op jit(solution)/shard_map/reduce_scatter | solution.py:38
  348.9 3.8 %copy.5 = f32[512,2,384]{2,1,0:T(2,128)} copy(f32[512,2,384]{2,0,1:T(8,128)} %reduce-scatter.2.cloned.1.call-done) | data formatting | bytes 3145728 | tf_op jit(solution)/shard_map/reduce_scatter | solution.py:38
Async XLA Ops:
  6.5 111.0 %all-gather.2.cloned.1.call-start = ((), (), s32[]{:S(2)}) async-start(), calls=%async_computation.1 | async-start | bytes 20971520 | tf_op jit(solution)/shard_map/all_gather | solution.py:36
  7.3 341.6 %reduce-scatter.2.cloned.1.call-start = ((), (), s32[]{:S(2)}) async-start(), calls=%async_computation.2 | async-start | bytes 14155776 | tf_op jit(solution)/shard_map/reduce_scatter | solution.py:38
  117.5 8.5 %copy-start = (bf16[2048,4096]{1,0:T(8,128)(2,1)S(1)}, bf16[2048,4096]{1,0:T(8,128)(2,1)}, u32[]{:S(2)}) copy-start(bf16[2048,4096]{1,0:T(8,128)(2,1)} %all-gather.2.cloned.1.call-done) | copy-start | bytes 50331652
  117.5 8.9 %copy-start.1 = (bf16[2048,384]{1,0:T(8,128)(2,1)S(1)}, bf16[2048,384]{1,0:T(8,128)(2,1)}, u32[]{:S(2)}) copy-start(bf16[2048,384]{1,0:T(8,128)(2,1)} %param.5) | copy-start | bytes 4718596
Sparse Core Ops, SparseCore 0:
  8.9 108.6 all-gather.1
  141.4 207.4 reduce-scatter.1
where the time goes:
time: 360 us; the launch traced here: 359 us
  waiting for transfers between devices  311 us (86%)
  between operations  17.3 us (5%)
  matrix products  14.2 us (4%)
  other arithmetic  9.47 us (3%)
  local copies, waits for them, and re-layouts  7.81 us (2%)
    reduce_scatter x1, waiting for transfers between devices, per_device(): return lax.psum_scatter(terms, 'dp', scatter_dimension=0, tiled=True)  208 us
    all_gather x1, waiting for transfers between devices, per_device(): whole = lax.all_gather(tokens, 'tensor', axis=1, tiled=True)  102 us
    dot_general x2, matrix products, block_term(): lax.dot_general(block_x, block_g, (((0,), (0,)), ((), ())), preferred_ele...  14.2 us
    another operation x1, other arithmetic, all_experts(): return jnp.stack(terms, 1)  8.12 us
  transfers between devices with their start and end apart: 2, of which 2 were waited for; matrix products, arithmetic and copies ran while one was open for 1% of the time, Pallas kernels for 0%

commit v1 on v0

v1 whole, which is shorter than its diff:
```python
import functools

import jax
import jax.numpy as jnp
from jax import lax
from jax.experimental import pallas as pl
from jax.experimental.pallas import tpu as pltpu
from jax.sharding import PartitionSpec as P

CAP = 1024
SUB = 128
MESH = pl.DeviceIdType.MESH


def block_term(columns, grads, lower, upper, size):
    total_rows = columns.shape[0]
    first = jnp.minimum(lower, total_rows - size)
    rows = first + jnp.arange(size, dtype=jnp.int32)
    keep = (rows >= lower) & (rows < upper)
    block_x = lax.dynamic_slice_in_dim(columns, first, size, 0)
    block_g = lax.dynamic_slice_in_dim(grads, first, size, 0)
    block_g = jnp.where(keep[:, None], block_g, jnp.zeros_like(block_g))
    return lax.dot_general(
        block_x, block_g, (((0,), (0,)), ((), ())), preferred_element_type=jnp.float32
    )


def plain_device(tokens, cotangent, seg_start, seg_length):
    whole = lax.all_gather(tokens, "tensor", axis=1, tiled=True)
    terms = []
    for expert in range(seg_start.shape[1]):
        start = seg_start[0, expert]
        upper = start + seg_length[0, expert]
        terms.append(block_term(whole, cotangent, start, upper, CAP))
    return lax.psum_scatter(jnp.stack(terms, 1), "dp", scatter_dimension=0, tiled=True)


def grad_kernel(
    n_dp, n_t, experts, tok_ref, cot_ref, info_ref, out_ref,
    cot_in, info_in, gt, tok, part, recv_r, recv_l,
    tok_send, tok_recv, small_send, small_recv, r_send, r_recv, l_send, l_recv,
):
    d = lax.axis_index("dp")
    t = lax.axis_index("tensor")
    line = n_dp // 2
    z, y = d // 2, d % 2
    rows, width = tok_ref.shape
    ff = cot_ref.shape[1]
    half = width // 2
    n_sub = half // SUB
    others = n_t // 2 - 1
    partner = (d, t + 1 - 2 * (t % 2))
    pair = (d + 1 - 2 * y, t)
    across = [(d, (t + 2 * k) % n_t) for k in range(1, others + 1)]

    barrier = pltpu.get_barrier_semaphore()
    for device in [partner, pair] + across:
        pl.semaphore_signal(barrier, inc=1, device_id=device, device_id_type=MESH)

    @pl.when(z > 0)
    def _():
        pl.semaphore_signal(barrier, inc=1, device_id=(d - 2, t), device_id_type=MESH)

    @pl.when(z < line - 1)
    def _():
        pl.semaphore_signal(barrier, inc=1, device_id=(d + 2, t), device_id_type=MESH)

    ends = jnp.where(z > 0, 1, 0) + jnp.where(z < line - 1, 1, 0)
    pl.semaphore_wait(barrier, 2 + others + ends)

    def slot(r, j, q):
        return tok.at[r, j, :, pl.ds(pl.multiple_of(q * SUB, SUB), SUB)]

    def own(parity, j):
        return tok_ref.at[:, pl.ds(pl.multiple_of(parity * half + j * SUB, SUB), SUB)]

    def send(src, r, q, j, kind, device):
        return pltpu.make_async_remote_copy(
            src_ref=src, dst_ref=slot(r, j, q), send_sem=tok_send.at[kind, j],
            recv_sem=tok_recv.at[r, q, j], device_id=device, device_id_type=MESH,
        )

    def arrived(r, q, j):
        send(slot(r, j, q), r, q, j, 0, partner).wait_recv()

    info_copy = pltpu.make_async_remote_copy(
        src_ref=info_ref, dst_ref=info_in, send_sem=small_send.at[0],
        recv_sem=small_recv.at[0], device_id=pair, device_id_type=MESH,
    )
    cot_copy = pltpu.make_async_remote_copy(
        src_ref=cot_ref, dst_ref=cot_in, send_sem=small_send.at[1],
        recv_sem=small_recv.at[1], device_id=pair, device_id_type=MESH,
    )
    info_copy.start()
    cot_copy.start()
    for j in range(n_sub):
        send(own(1 - y, j), 1, t, j, 1, pair).start()
        for k, device in enumerate(across):
            send(own(y, j), 0, t, j, 3 + 4 * k, device).start()
        send(own(y, j), 0, t, j, 0, partner).start()
    for j in range(n_sub):
        tok[0, j, :, pl.ds(pl.multiple_of(t * SUB, SUB), SUB)] = tok_ref[
            :, pl.ds(pl.multiple_of(y * half + j * SUB, SUB), SUB)
        ]

    chunk = 256

    def masked(r, grads, info):
        @pl.loop(0, rows // chunk)
        def _(i):
            at = pl.ds(pl.multiple_of(i * chunk, chunk), chunk)
            block = grads[at, :].astype(jnp.float32).T
            col = i * chunk + lax.broadcasted_iota(jnp.int32, (ff, chunk), 1)
            for e in range(experts):
                keep = (col >= info[2 * e : 2 * e + 1, :]) & (col < info[2 * e + 1 : 2 * e + 2, :])
                gt[r, e * ff : (e + 1) * ff, at] = jnp.where(keep, block, 0.0).astype(gt.dtype)

    masked(0, cot_ref, info_ref)
    info_copy.wait_recv()
    cot_copy.wait_recv()
    masked(1, cot_in, info_in)

    def from_pair(j):
        arrived(1, t, j)
        for k, device in enumerate(across):
            send(slot(1, j, t), 1, t, j, 4 + 4 * k, device).start()
        send(slot(1, j, t), 1, t, j, 2, partner).start()

    def right(j, q):
        return pltpu.make_async_remote_copy(
            src_ref=part.at[j, q], dst_ref=recv_r.at[j, q], send_sem=r_send.at[j, q],
            recv_sem=r_recv.at[j, q], device_id=(d + 2, t), device_id_type=MESH,
        )

    def left(j, q):
        return pltpu.make_async_remote_copy(
            src_ref=part.at[j, q], dst_ref=recv_l.at[j, q], send_sem=l_send.at[j, q],
            recv_sem=l_recv.at[j, q], device_id=(d - 2, t), device_id_type=MESH,
        )

    tile = 256
    from_pair(0)

    @pl.loop(0, n_sub)
    def _(j):
        @pl.when(j + 1 < n_sub)
        def _():
            from_pair(j + 1)

        for r in range(2):
            for k in range(others):
                q = (t + 2 * (k + 1)) % n_t
                arrived(r, q, j)
                send(slot(r, j, q), r, q, j, 5 + 4 * k + r, partner).start()
        for r in range(2):
            for k in range(others + 1):
                arrived(r, (partner[1] + 2 * k) % n_t, j)

        @pl.loop(0, experts * ff // tile)
        def _(m):
            at = pl.ds(pl.multiple_of(m * tile, tile), tile)
            total = jnp.dot(gt[0, at, :], tok[0, j], preferred_element_type=jnp.float32)
            total += jnp.dot(gt[1, at, :], tok[1, j], preferred_element_type=jnp.float32)
            for q in range(n_t):
                part[j, q, at, :] = total[:, q * SUB : (q + 1) * SUB]

        for q in range(n_t):
            @pl.when((z == line - 1) & (q < z))
            def _():
                left(j, q).start()
        for q in reversed(range(n_t)):
            @pl.when((z == 0) & (q > z))
            def _():
                right(j, q).start()

    @pl.loop(0, n_sub)
    def _(j):
        order = []
        for q in range(n_t):
            for o in (n_t - 1 - q, q):
                if o not in order:
                    order.append(o)
        for q in order:
            @pl.when((q > z) & (z > 0))
            def _():
                right(j, q).wait_recv()
                part[j, q] = part[j, q] + recv_r[j, q]
                right(j, q).start()

            @pl.when((q < z) & (z < line - 1))
            def _():
                left(j, q).wait_recv()
                part[j, q] = part[j, q] + recv_l[j, q]
                left(j, q).start()

    @pl.loop(0, n_sub)
    def _(j):
        out_ref[j] = part[j, z]

        @pl.when(z > 0)
        def _():
            right(j, z).wait_recv()
            out_ref[j] += recv_r[j, z]

        @pl.when(z < line - 1)
        def _():
            left(j, z).wait_recv()
            out_ref[j] += recv_l[j, z]

    @pl.loop(0, n_sub)
    def _(j):
        for q in range(n_t):
            @pl.when(q > z)
            def _():
                right(j, q).wait_send()

            @pl.when(q < z)
            def _():
                left(j, q).wait_send()
        for kind in range(3 + 4 * others):
            send(slot(0, j, t), 0, t, j, kind, partner).wait_send()
    info_copy.wait_send()
    cot_copy.wait_send()


def kernel_device(n_dp, n_t, tokens, cotangent, seg_start, seg_length):
    rows, width = tokens.shape
    ff = cotangent.shape[1]
    experts = seg_start.shape[1]
    half = width // 2
    n_sub = half // SUB
    others = n_t // 2 - 1
    bounds = jnp.stack([seg_start[0], seg_start[0] + seg_length[0]], 1).reshape(-1)
    pad = -(2 * experts) % 8
    info = jnp.broadcast_to(jnp.pad(bounds, (0, pad))[:, None], (2 * experts + pad, 256))
    dma = pltpu.SemaphoreType.DMA
    blocks = (n_sub, n_t, experts * ff, SUB)
    vmem = pl.BlockSpec(memory_space=pltpu.VMEM)
    out = pl.pallas_call(
        functools.partial(grad_kernel, n_dp, n_t, experts),
        out_shape=jax.ShapeDtypeStruct((n_sub, experts * ff, SUB), jnp.float32),
        in_specs=[vmem] * 3,
        out_specs=vmem,
        scratch_shapes=[
            pltpu.VMEM((rows, ff), cotangent.dtype),
            pltpu.VMEM(info.shape, jnp.int32),
            pltpu.VMEM((2, experts * ff, rows), cotangent.dtype),
            pltpu.VMEM((2, n_sub, rows, n_t * SUB), tokens.dtype),
            pltpu.VMEM(blocks, jnp.float32),
            pltpu.VMEM(blocks, jnp.float32),
            pltpu.VMEM(blocks, jnp.float32),
            dma((3 + 4 * others, n_sub)),
            dma((2, n_t, n_sub)),
            dma((2,)),
            dma((2,)),
            dma((n_sub, n_t)),
            dma((n_sub, n_t)),
            dma((n_sub, n_t)),
            dma((n_sub, n_t)),
        ],
        compiler_params=pltpu.CompilerParams(
            collective_id=0, has_side_effects=True, vmem_limit_bytes=67043328
        ),
    )(tokens, cotangent, info)
    out = out.reshape(n_sub, experts, ff, SUB)
    return out.transpose(0, 3, 1, 2).reshape(half, experts, ff)


def solution(mesh):
    n_dp, n_t = mesh.shape["dp"], mesh.shape["tensor"]
    body = plain_device
    if n_dp == 2 * n_t:
        body = functools.partial(kernel_device, n_dp, n_t)
    in_specs = (P("dp", "tensor"), P("dp", "tensor"), P("dp", None), P("dp", None))
    out_specs = P("dp", None, "tensor")
    return jax.shard_map(
        body, mesh=mesh, in_specs=in_specs, out_specs=out_specs, check_vma=False
    )
```

time: 360 us -> 227 us (0.63)
  waiting for transfers between devices: 311 us -> 0 us
  Pallas kernels: 0 us -> 221 us
  between operations: 17.3 us -> 0.01 us
  matrix products: 14.2 us -> 0 us
  other arithmetic: 9.47 us -> 1.34 us
    pallas_call x0 -> x1, Pallas kernels: none -> 221 us  [kernel_device(): pl.pallas_call(functools.partial(grad_kernel, n_dp, n_t, experts), out_sh...]
    reduce_scatter x1 -> x0, waiting for transfers between devices: 208 us -> none  [per_device(): return lax.psum_scatter(terms, 'dp', scatter_dimension=0, tiled=True)]
    all_gather x1 -> x0, waiting for transfers between devices: 102 us -> none  [per_device(): whole = lax.all_gather(tokens, 'tensor', axis=1, tiled=True)]
    dot_general x2 -> x0, matrix products: 14.2 us -> none  [block_term(): lax.dot_general(block_x, block_g, (((0,), (0,)), ((), ())), preferred_ele...]
    another operation x1, other arithmetic: 8.12 us -> 0.66 us  [kernel_device(): jnp.stack([seg_start[0], seg_start[0] + seg_length[0]], 1).reshape(-1)]
    reduce_scatter x1 -> x0, local copies, waits for them, and re-layouts: 3.76 us -> none  [per_device(): return lax.psum_scatter(terms, 'dp', scatter_dimension=0, tiled=True)]
    transpose x0 -> x1, local copies, waits for them, and re-layouts: none -> 3.68 us  [kernel_device(): return out.transpose(0, 3, 1, 2).reshape(half, experts, ff)]
  transfers between devices with their start and end apart: 2 -> 0, of which waited for: 2 -> 0; matrix products, arithmetic and copies ran while one was open for 1% -> 0% of each run, Pallas kernels for 0% -> 0%
where the time goes in v1:
time: 227 us
  Pallas kernels  221 us (97%)
  local copies, waits for them, and re-layouts  4.53 us (2%)
    pallas_call x1, Pallas kernels, kernel_device(): pl.pallas_call(functools.partial(grad_kernel, n_dp, n_t, experts), out_sh...  221 us

profile of v1, /device:TPU:0, one launch (start us, length us, event | category | flops | bytes accessed | tf_op | source)
XLA Modules:
  0.0 226.9 jit_solution(16115060145149893360)
XLA Ops:
  0.0 0.7 bitcast_add_fusion
  0.7 0.7 pad_add_fusion
  1.3 0.1 copy.5
  1.4 0.1 reshape.27
  1.5 0.7 broadcast_in_dim.2.info_ref
  2.2 221.0 %shard_map.46 = f32[4,768,128]{2,1,0:T(8,128)} custom-call(bf16[2048,1024]{1,0:T(8,128)(2,1)} %tok_ref.1, bf16[2048,384]{1,0:T(8,128)(2,1)} %cot_ref.1, s32[8,256]{1,0:T(8,128)} %broadcast_in_dim.2.info_ref), custom_call_target="tpu_custom_call" | custom-call | tf_op jit(solution)/shard_map/pallas_call | solution.py:239
  223.2 3.7 %copy.6 = f32[4,128,2,384]{3,2,1,0:T(2,128)} copy(f32[4,128,2,384]{1,3,2,0:T(8,128)} %bitcast.8) | data formatting | bytes 3145728 | tf_op jit(solution)/shard_map/transpose | solution.py:266
  (1 shorter events, 0.0 us)

commit v2 on v1

v2 whole, which is shorter than its diff:
```python
import functools

import jax
import jax.numpy as jnp
from jax import lax
from jax.experimental import pallas as pl
from jax.experimental.pallas import tpu as pltpu
from jax.sharding import PartitionSpec as P

CAP = 1024
SUB = 128
MESH = pl.DeviceIdType.MESH


def block_term(columns, grads, lower, upper, size):
    total_rows = columns.shape[0]
    first = jnp.minimum(lower, total_rows - size)
    rows = first + jnp.arange(size, dtype=jnp.int32)
    keep = (rows >= lower) & (rows < upper)
    block_x = lax.dynamic_slice_in_dim(columns, first, size, 0)
    block_g = lax.dynamic_slice_in_dim(grads, first, size, 0)
    block_g = jnp.where(keep[:, None], block_g, jnp.zeros_like(block_g))
    return lax.dot_general(
        block_x, block_g, (((0,), (0,)), ((), ())), preferred_element_type=jnp.float32
    )


def plain_device(tokens, cotangent, seg_start, seg_length):
    whole = lax.all_gather(tokens, "tensor", axis=1, tiled=True)
    terms = []
    for expert in range(seg_start.shape[1]):
        start = seg_start[0, expert]
        upper = start + seg_length[0, expert]
        terms.append(block_term(whole, cotangent, start, upper, CAP))
    return lax.psum_scatter(jnp.stack(terms, 1), "dp", scatter_dimension=0, tiled=True)


def plan(n_sub, n_ff):
    events = []
    for i in range(max(n_sub, n_ff)):
        events += [("cot", i)] * (i < n_ff) + [("tok", i)] * (i < n_sub)
    groups = []
    for kind, i in events:
        if kind == "tok":
            groups.append((i, []))
    have = {i: max(0, min(n_ff, i + 2)) for i in range(n_sub)}
    seen = set()
    for i, added in groups:
        for j in range(i + 1):
            for f in range(have[i]):
                if (j, f) not in seen:
                    seen.add((j, f))
                    added.append((j, f))
    for j in range(n_sub):
        for f in range(n_ff):
            if (j, f) not in seen:
                groups[-1][1].append((j, f))
    return events, groups, have


def grad_kernel(
    n_dp, n_t, experts, tok_ref, cot_ref, info_ref, out_ref,
    cot_in, info_in, gt, tok, part, recv_r, recv_l,
    tok_send, tok_recv, small_send, small_recv, r_send, r_recv, l_send, l_recv,
):
    d = lax.axis_index("dp")
    t = lax.axis_index("tensor")
    line = n_dp // 2
    z, y = d // 2, d % 2
    rows, width = tok_ref.shape
    ff = cot_ref.shape[1]
    half = width // 2
    n_sub, n_ff = half // SUB, ff // SUB
    n_steps = n_sub * n_ff
    others = n_t // 2 - 1
    partner = (d, t + 1 - 2 * (t % 2))
    pair = (d + 1 - 2 * y, t)
    across = [(d, (t + 2 * k) % n_t) for k in range(1, others + 1)]

    barrier = pltpu.get_barrier_semaphore()
    for device in [partner, pair] + across:
        pl.semaphore_signal(barrier, inc=1, device_id=device, device_id_type=MESH)

    @pl.when(z > 0)
    def _():
        pl.semaphore_signal(barrier, inc=1, device_id=(d - 2, t), device_id_type=MESH)

    @pl.when(z < line - 1)
    def _():
        pl.semaphore_signal(barrier, inc=1, device_id=(d + 2, t), device_id_type=MESH)

    ends = jnp.where(z > 0, 1, 0) + jnp.where(z < line - 1, 1, 0)
    pl.semaphore_wait(barrier, 2 + others + ends)

    def slot(r, j, q):
        return tok.at[r, j, :, pl.ds(pl.multiple_of(q * SUB, SUB), SUB)]

    def own(parity, j):
        return tok_ref.at[:, pl.ds(pl.multiple_of(parity * half + j * SUB, SUB), SUB)]

    def send(src, r, q, j, kind, device):
        return pltpu.make_async_remote_copy(
            src_ref=src, dst_ref=slot(r, j, q), send_sem=tok_send.at[kind, j],
            recv_sem=tok_recv.at[r, q, j], device_id=device, device_id_type=MESH,
        )

    def arrived(r, q, j):
        send(slot(r, j, q), r, q, j, 0, partner).wait_recv()

    info_copy = pltpu.make_async_remote_copy(
        src_ref=info_ref, dst_ref=info_in, send_sem=small_send.at[n_ff],
        recv_sem=small_recv.at[n_ff], device_id=pair, device_id_type=MESH,
    )

    def cot_copy(f):
        at = pl.ds(f * SUB, SUB)
        return pltpu.make_async_remote_copy(
            src_ref=cot_ref.at[:, at], dst_ref=cot_in.at[:, at], send_sem=small_send.at[f],
            recv_sem=small_recv.at[f], device_id=pair, device_id_type=MESH,
        )

    def own_across(j):
        for k, device in enumerate(across):
            send(own(y, j), 0, t, j, 3 + 4 * k, device).start()

    events, groups, have = plan(n_sub, n_ff)
    info_copy.start()
    for kind, i in events:
        if kind == "cot":
            cot_copy(i).start()
        else:
            send(own(1 - y, i), 1, t, i, 1, pair).start()
    for j in range(min(2, n_sub)):
        own_across(j)
    for j in range(n_sub):
        send(own(y, j), 0, t, j, 0, partner).start()
    for j in range(n_sub):
        tok[0, j, :, pl.ds(pl.multiple_of(t * SUB, SUB), SUB)] = tok_ref[
            :, pl.ds(pl.multiple_of(y * half + j * SUB, SUB), SUB)
        ]

    chunk = 256
    deep = experts * SUB

    def masked(r, grads, info, f):
        @pl.loop(0, rows // chunk)
        def _(i):
            at = pl.ds(pl.multiple_of(i * chunk, chunk), chunk)
            block = grads[at, f * SUB : (f + 1) * SUB].astype(jnp.float32).T
            col = i * chunk + lax.broadcasted_iota(jnp.int32, (SUB, chunk), 1)
            for e in range(experts):
                keep = (col >= info[2 * e : 2 * e + 1, :]) & (col < info[2 * e + 1 : 2 * e + 2, :])
                gt[r, f * deep + e * SUB : f * deep + (e + 1) * SUB, at] = jnp.where(
                    keep, block, 0.0
                ).astype(gt.dtype)

    for f in range(n_ff):
        masked(0, cot_ref, info_ref, f)
    info_copy.wait_recv()

    def right(s, q):
        return pltpu.make_async_remote_copy(
            src_ref=part.at[s, q], dst_ref=recv_r.at[s, q], send_sem=r_send.at[s, q],
            recv_sem=r_recv.at[s, q], device_id=(d + 2, t), device_id_type=MESH,
        )

    def left(s, q):
        return pltpu.make_async_remote_copy(
            src_ref=part.at[s, q], dst_ref=recv_l.at[s, q], send_sem=l_send.at[s, q],
            recv_sem=l_recv.at[s, q], device_id=(d - 2, t), device_id_type=MESH,
        )

    def middle(s):
        u, v = s - (z - 1), s - (line - 2 - z)
        for q in reversed(range(n_t)):
            @pl.when((q > z) & (z > 0) & (u >= 0) & (u < n_steps))
            def _():
                right(u, q).wait_recv()
                part[u, q] = part[u, q] + recv_r[u, q]
                right(u, q).start()
        for q in range(n_t):
            @pl.when((q < z) & (z < line - 1) & (v >= 0) & (v < n_steps))
            def _():
                left(v, q).wait_recv()
                part[v, q] = part[v, q] + recv_l[v, q]
                left(v, q).start()

    def from_pair(j):
        arrived(1, t, j)
        for k, device in enumerate(across):
            send(slot(1, j, t), 1, t, j, 4 + 4 * k, device).start()
        send(slot(1, j, t), 1, t, j, 2, partner).start()
        if j + 2 < n_sub:
            own_across(j + 2)

    def from_across(r, j):
        for k in range(others):
            q = (t + 2 * (k + 1)) % n_t
            arrived(r, q, j)
            send(slot(r, j, q), r, q, j, 5 + 4 * k + r, partner).start()

    blocks_in, subs_in, s, hops = 0, 0, 0, 0
    places = []
    last = []
    for i, steps in groups:
        for j in range(subs_in, min(n_sub, i + 1 + (blocks_in == n_ff))):
            while blocks_in < min(n_ff, j + 1):
                cot_copy(blocks_in).wait_recv()
                masked(1, cot_in, info_in, blocks_in)
                blocks_in += 1
            from_pair(j)
            from_across(0, j)
            subs_in = j + 1
        while blocks_in < have[i]:
            cot_copy(blocks_in).wait_recv()
            masked(1, cot_in, info_in, blocks_in)
            blocks_in += 1
        from_across(1, i)
        for r in range(2):
            for k in range(others + 1):
                arrived(r, (partner[1] + 2 * k) % n_t, i)
        for j, f in steps:
            at = pl.ds(f * deep, deep)
            total = jnp.dot(gt[0, at, :], tok[0, j], preferred_element_type=jnp.float32)
            total += jnp.dot(gt[1, at, :], tok[1, j], preferred_element_type=jnp.float32)
            for q in range(n_t):
                part[s, q] = total[:, q * SUB : (q + 1) * SUB]
            for q in range(n_t):
                @pl.when((z == line - 1) & (q < z))
                def _():
                    left(s, q).start()
            for q in reversed(range(n_t)):
                @pl.when((z == 0) & (q > z))
                def _():
                    right(s, q).start()
            places.append((j, f))
            s += 1
        last.append(s)
        if len(last) > 1:
            pl.loop(hops, last[-2])(middle)
            hops = last[-2]
    pl.loop(hops, n_steps + line - 2)(middle)

    for s, (j, f) in enumerate(places):
        here = j * n_ff + f
        out_ref[here] = part[s, z]

        @pl.when(z > 0)
        def _():
            right(s, z).wait_recv()
            out_ref[here] += recv_r[s, z]

        @pl.when(z < line - 1)
        def _():
            left(s, z).wait_recv()
            out_ref[here] += recv_l[s, z]

    @pl.loop(0, n_steps)
    def _(s):
        for q in range(n_t):
            @pl.when(q > z)
            def _():
                right(s, q).wait_send()

            @pl.when(q < z)
            def _():
                left(s, q).wait_send()

    @pl.loop(0, n_sub)
    def _(j):
        for kind in range(3 + 4 * others):
            send(slot(0, j, t), 0, t, j, kind, partner).wait_send()
    for f in range(n_ff):
        cot_copy(f).wait_send()
    info_copy.wait_send()


def kernel_device(n_dp, n_t, tokens, cotangent, seg_start, seg_length):
    rows, width = tokens.shape
    ff = cotangent.shape[1]
    experts = seg_start.shape[1]
    half = width // 2
    n_sub = half // SUB
    others = n_t // 2 - 1
    bounds = jnp.stack([seg_start[0], seg_start[0] + seg_length[0]], 1).reshape(-1)
    pad = -(2 * experts) % 8
    info = jnp.broadcast_to(jnp.pad(bounds, (0, pad))[:, None], (2 * experts + pad, 256))
    dma = pltpu.SemaphoreType.DMA
    n_ff = ff // SUB
    blocks = (n_sub * n_ff, n_t, experts * SUB, SUB)
    vmem = pl.BlockSpec(memory_space=pltpu.VMEM)
    out = pl.pallas_call(
        functools.partial(grad_kernel, n_dp, n_t, experts),
        out_shape=jax.ShapeDtypeStruct((n_sub * n_ff, experts * SUB, SUB), jnp.float32),
        in_specs=[vmem] * 3,
        out_specs=vmem,
        scratch_shapes=[
            pltpu.VMEM((rows, ff), cotangent.dtype),
            pltpu.VMEM(info.shape, jnp.int32),
            pltpu.VMEM((2, experts * ff, rows), cotangent.dtype),
            pltpu.VMEM((2, n_sub, rows, n_t * SUB), tokens.dtype),
            pltpu.VMEM(blocks, jnp.float32),
            pltpu.VMEM(blocks, jnp.float32),
            pltpu.VMEM(blocks, jnp.float32),
            dma((3 + 4 * others, n_sub)),
            dma((2, n_t, n_sub)),
            dma((n_ff + 1,)),
            dma((n_ff + 1,)),
            dma((n_sub * n_ff, n_t)),
            dma((n_sub * n_ff, n_t)),
            dma((n_sub * n_ff, n_t)),
            dma((n_sub * n_ff, n_t)),
        ],
        compiler_params=pltpu.CompilerParams(
            collective_id=0, has_side_effects=True, vmem_limit_bytes=67043328
        ),
    )(tokens, cotangent, info)
    out = out.reshape(n_sub, n_ff, experts, SUB, SUB)
    return out.transpose(0, 4, 2, 1, 3).reshape(half, experts, ff)


def solution(mesh):
    n_dp, n_t = mesh.shape["dp"], mesh.shape["tensor"]
    body = plain_device
    if n_dp == 2 * n_t:
        body = functools.partial(kernel_device, n_dp, n_t)
    in_specs = (P("dp", "tensor"), P("dp", "tensor"), P("dp", None), P("dp", None))
    out_specs = P("dp", None, "tensor")
    return jax.shard_map(
        body, mesh=mesh, in_specs=in_specs, out_specs=out_specs, check_vma=False
    )
```

time: 227 us -> 172 us (0.76)
  Pallas kernels: 221 us -> 163 us
    pallas_call x1, Pallas kernels: 221 us -> 163 us  [kernel_device(): pl.pallas_call(functools.partial(grad_kernel, n_dp, n_t, experts), out_sh...]
    reshape x0 -> x3, local copies, waits for them, and re-layouts: none -> 5.14 us  [the longest x2 2.71 us: kernel_device(): return out.transpose(0, 4, 2, 1, 3).reshape(half, experts, ff)]
    transpose x1 -> x0, local copies, waits for them, and re-layouts: 3.68 us -> none  [kernel_device(): return out.transpose(0, 3, 1, 2).reshape(half, experts, ff)]
where the time goes in v2:
time: 172 us; the launch traced here: 171 us
  Pallas kernels  163 us (95%)
  local copies, waits for them, and re-layouts  5.99 us (3%)
    pallas_call x1, Pallas kernels, kernel_device(): pl.pallas_call(functools.partial(grad_kernel, n_dp, n_t, experts), out_sh...  163 us

profile of v2, /device:TPU:0, one launch (start us, length us, event | category | flops | bytes accessed | tf_op | source)
XLA Modules:
  0.0 170.6 jit_solution(14131371801241998590)
XLA Ops:
  0.0 0.7 bitcast_add_fusion
  0.7 0.7 pad_add_fusion
  1.3 0.1 copy.7
  1.4 0.1 reshape.27
  1.5 0.7 broadcast_in_dim.2.info_ref
  2.2 163.3 %shard_map.46 = f32[12,256,128]{2,1,0:T(8,128)} custom-call(bf16[2048,1024]{1,0:T(8,128)(2,1)} %tok_ref.1, bf16[2048,384]{1,0:T(8,128)(2,1)} %cot_ref.1, s32[8,256]{1,0:T(8,128)} %broadcast_in_dim.2.info_ref), custom_call_target="tpu_custom_call" | custom-call | tf_op jit(solution)/shard_map/pallas_call | solution.py:292
  165.5 2.4 %copy.11 = f32[4,3,2,128,128]{4,0,3,1,2:T(4,128)S(1)} copy(f32[4,3,2,128,128]{4,3,2,1,0:T(8,128)} %bitcast.11) | data formatting | bytes 3145728 | tf_op jit(solution)/shard_map/reshape | solution.py:318
  167.9 0.6 reshape.29
  168.5 2.1 %copy.9 = f32[512,2,384]{2,1,0:T(2,128)} copy(f32[512,2,384]{0,2,1:T(8,128)S(1)} %reshape.29) | data formatting | bytes 3145728 | tf_op jit(solution)/shard_map/reshape | solution.py:319
  (1 shorter events, 0.0 us)
